TPU v7x, 32 devices: a whole 2x2x4 slice. The times are simulated.
32 devices in a mesh: head: 8 (over z, y), ctx: 4 (over x, core).
Axes of the slice: x: 2, y: 2, z: 4, core: 2. Of those that a mesh axis runs over, the one named last changes fastest.
Arguments:
- query: bfloat16 [3072, 4096], P(('ctx', 'head')), may hold values from -8 to 8
- key: bfloat16 [3072, 2048], P(('ctx', 'head')), may hold values from -8 to 8
- value: bfloat16 [3072, 2048], P(('ctx', 'head')), may hold values from -8 to 8
- block_order: int32 [8], replicated, may hold values from 0 to 7, each once
Outputs:
- attended: bfloat16 [3072, 4096], P('ctx', 'head')
Inputs may be any that keep to these rules, and one draw needn't show every extreme that they name: `block_order`: each storage block index 0 to 7 appears exactly once.
All inputs are finite; a program needn't handle non-finite values.
Results may differ from a plain program's by a relative error of at most 0.0049.
Values may be sent and summed in bfloat16 or wider, within the bound.
A program may use at most 128 MiB of HBM per device.

v0:
```python
import functools
import math

import jax
import jax.numpy as jnp
from jax import lax
from jax.experimental import pallas as pl
from jax.experimental.pallas import tpu as pltpu
from jax.sharding import PartitionSpec as P

HEAD_WIDTH = 128
MESH = pl.DeviceIdType.MESH
CAP = 50.0
IN_SCALE = 1.0 / (12.0 * CAP)
OUT_SCALE = CAP * math.log2(math.e)
HIDDEN = -4096.0


def flip(index, step, size):
    out, bit = 0, 1
    while bit < size:
        mine = (index // bit) % 2
        turn = (step // bit) % 2
        out = out + (mine + turn - 2 * mine * turn) * bit
        bit *= 2
    return out


def kernel(
    n_head, n_ctx, pair,
    order, query, key, value, out,
    qbuf, kv, acc,
    q_send, k_send, v_send, q_recv, k_recv, v_recv,
    local_sem, f_send, r_send, f_recv,
):
    me = lax.axis_index("head")
    ctx = lax.axis_index("ctx")
    chip, core = ctx // 2, ctx % 2
    partner = chip * 2 + 1 - core
    chips = n_ctx // 2
    pieces = n_head // pair
    rows = query.shape[0]
    total = rows * n_head
    block = total // 2
    q_cols = query.shape[1] // n_head
    kv_cols = key.shape[1] // n_head
    kv_heads = kv_cols // HEAD_WIDTH
    per_kv = q_cols // kv_cols
    piece_rows = rows * pair
    same_core = [((chip + t) % chips) * 2 + core for t in range(1, chips)]
    peers = [flip(me, j, n_head) for j in range(1, n_head)]

    barrier = pltpu.get_barrier_semaphore()
    for d in peers:
        pl.semaphore_signal(barrier, inc=1, device_id={"head": d}, device_id_type=MESH)
    for c in [partner] + same_core:
        pl.semaphore_signal(barrier, inc=1, device_id={"ctx": c}, device_id_type=MESH)

    def rows_of(s):
        return pl.ds(pl.multiple_of(s * rows, rows), rows)

    def cols_of(s, width):
        return pl.ds(pl.multiple_of(s * width, width), width)

    mine = [
        pltpu.make_async_copy(key.at[:, cols_of(me, kv_cols)], kv.at[ctx, 0, rows_of(me)], local_sem.at[0]),
        pltpu.make_async_copy(value.at[:, cols_of(me, kv_cols)], kv.at[ctx, 1, rows_of(me)], local_sem.at[1]),
        pltpu.make_async_copy(query.at[:, cols_of(me, q_cols)], qbuf.at[rows_of(me)], local_sem.at[2]),
    ]
    for copy in mine:
        copy.start()

    pl.semaphore_wait(barrier, n_head - 1 + chips)

    def to_head(src, width, dst, send, recv, d):
        return pltpu.make_async_remote_copy(
            src_ref=src.at[:, cols_of(d, width)], dst_ref=dst.at[rows_of(me)],
            send_sem=send.at[d], recv_sem=recv.at[me],
            device_id={"head": d}, device_id_type=MESH,
        )

    near = n_head // 2
    sends = []
    for some in (peers[: near - 1], peers[near - 1 :]):
        for d in some:
            sends.append(to_head(key, kv_cols, kv.at[ctx, 0], k_send, k_recv, d))
            sends.append(to_head(value, kv_cols, kv.at[ctx, 1], v_send, v_recv, d))
        for d in some:
            sends.append(to_head(query, q_cols, qbuf, q_send, q_recv, d))
    for copy in sends:
        copy.start()

    def arrived(dst, recv, s):
        pltpu.make_async_copy(dst.at[rows_of(s)], dst.at[rows_of(s)], recv.at[s]).wait()

    def piece_ref(c, p):
        return kv.at[c, :, pl.ds(pl.multiple_of(p * piece_rows, piece_rows), piece_rows)]

    def forward(c, p, dest, send):
        return pltpu.make_async_remote_copy(
            src_ref=piece_ref(c, p), dst_ref=piece_ref(c, p),
            send_sem=send, recv_sem=f_recv.at[c, p],
            device_id={"ctx": dest}, device_id_type=MESH,
        )

    def piece_arrived(c, p):
        pltpu.make_async_copy(piece_ref(c, p), piece_ref(c, p), f_recv.at[c, p]).wait()

    passed = []

    def relay(p):
        for c in same_core:
            piece_arrived(c, p)
            copy = forward(c, p, partner, r_send.at[c, p])
            copy.start()
            passed.append(copy)

    home = me // pair
    near_pieces = pieces // 2
    near_half = home // near_pieces

    def collect(step):
        p = flip(home, step, pieces)
        for t in range(pair):
            s = flip(me, step * pair + t, n_head)
            if step == 0 and t == 0:
                mine[0].wait()
                mine[1].wait()
            else:
                arrived(kv.at[ctx, 0], k_recv, s)
                arrived(kv.at[ctx, 1], v_recv, s)
        for dest in same_core + [partner]:
            copy = forward(ctx, p, dest, f_send.at[dest, p])
            copy.start()
            passed.append(copy)

    def others_arrived(t, steps):
        c = ((chip + t) % chips) * 2 + 1 - core
        for step in steps:
            piece_arrived(c, flip(home, step, pieces))

    ones = jnp.ones((2 * block, HEAD_WIDTH), jnp.bfloat16)

    def unit(step, far, t, diagonal):
        g = flip(home, step, pieces)
        first_row = g * piece_rows
        q_half = first_row // block
        q_block = order[2 * ctx + q_half]
        half = near_half + far - 2 * near_half * far
        c0 = ((chip + t) % chips) * 2 + core
        c1 = ((chip + t) % chips) * 2 + 1 - core
        q_span = pl.ds(pl.multiple_of(first_row, piece_rows), piece_rows)
        k_span = pl.ds(pl.multiple_of(half * block, block), block)
        low = jnp.where(order[2 * c0 + half] <= q_block, 0.0, HIDDEN)
        high = jnp.where(order[2 * c1 + half] <= q_block, 0.0, HIDDEN)
        for h in range(kv_heads):
            cols = slice(h * HEAD_WIDTH, (h + 1) * HEAD_WIDTH)
            q = jnp.concatenate(
                [qbuf[q_span, (h * per_kv + i) * HEAD_WIDTH : (h * per_kv + i + 1) * HEAD_WIDTH] for i in range(per_kv)],
                axis=0,
            )
            k = jnp.concatenate([kv[c0, 0, k_span, cols], kv[c1, 0, k_span, cols]], axis=0)
            v = jnp.concatenate([kv[c0, 1, k_span, cols], kv[c1, 1, k_span, cols]], axis=0)
            x = lax.dot_general(q, k, (((1,), (1,)), ((), ())), preferred_element_type=jnp.float32)
            x = jnp.tanh(x * IN_SCALE) * OUT_SCALE
            if diagonal:
                q_at = first_row - q_half * block + lax.broadcasted_iota(jnp.int32, (piece_rows, block), 0)
                visible = lax.broadcasted_iota(jnp.int32, (piece_rows, block), 1) <= q_at
                e = jnp.exp2(x[:, :block]).reshape(per_kv, piece_rows, block)
                left = jnp.where(visible[None], e, 0.0).reshape(per_kv * piece_rows, block)
            else:
                left = jnp.exp2(x[:, :block] + low)
            w = jnp.concatenate([left, jnp.exp2(x[:, block:] + high)], axis=1).astype(jnp.bfloat16)
            o = jnp.dot(w, jnp.concatenate([v, ones], axis=1), preferred_element_type=jnp.float32)
            if diagonal:
                acc[step, h] = o
            else:
                acc[step, h] += o

    def q_arrived(step):
        for t in range(pair):
            j = step * pair + t

            @pl.when(j > 0)
            def _():
                arrived(qbuf, q_recv, flip(me, j, n_head))

    def finish(step):
        first_row = flip(home, step, pieces) * piece_rows
        span = pl.ds(pl.multiple_of(first_row, piece_rows), piece_rows)
        for h in range(kv_heads):
            a = acc[step, h]
            o = (a[:, :HEAD_WIDTH] / a[:, HEAD_WIDTH:]).astype(jnp.bfloat16)
            for i in range(per_kv):
                at = (h * per_kv + i) * HEAD_WIDTH
                out[span, at : at + HEAD_WIDTH] = o[i * piece_rows : (i + 1) * piece_rows]

    def each(count, body):
        lax.fori_loop(0, count, lambda i, carry: (body(i), carry)[1], 0)

    near_steps, far_steps = range(near_pieces), range(near_pieces, pieces)
    for step in near_steps:
        collect(step)
    for step in near_steps:
        relay(flip(home, step, pieces))
    mine[2].wait()
    for t in range(chips):
        others_arrived(t, near_steps)

    def near_near(step):
        q_arrived(step)
        unit(step, 0, 0, True)
        each(chips - 1, lambda t: unit(step, 0, t + 1, False))

    each(near_pieces, near_near)
    for step in far_steps:
        collect(step)
        if step > near_pieces:
            relay(flip(home, step - 1, pieces))
    others_arrived(0, far_steps)
    each(near_pieces, lambda step: unit(step, 1, 0, False))
    relay(flip(home, pieces - 1, pieces))
    for t in range(1, chips):
        others_arrived(t, far_steps)

    def rest(step):
        each(chips - 1, lambda t: unit(step, 1, t + 1, False))
        finish(step)

    each(near_pieces, rest)

    def far_all(i):
        step = near_pieces + i
        q_arrived(step)
        unit(step, 1, 0, True)
        each(2 * chips - 1, lambda u: unit(step, u // chips, u % chips + u // chips, False))
        finish(step)

    each(near_pieces, far_all)
    for copy in sends:
        copy.wait_send()
    for copy in passed:
        copy.wait_send()


def shards(n_head, n_ctx, query, key, value, block_order):
    rows = query.shape[0]
    total = rows * n_head
    q_cols = query.shape[1] // n_head
    kv_cols = key.shape[1] // n_head
    kv_heads = kv_cols // HEAD_WIDTH
    per_kv = q_cols // kv_cols
    pair = 2
    pieces = n_head // pair
    hbm = pl.BlockSpec(memory_space=pltpu.HBM)
    dma = pltpu.SemaphoreType.DMA
    return pl.pallas_call(
        functools.partial(kernel, n_head, n_ctx, pair),
        out_shape=jax.ShapeDtypeStruct((total, q_cols), jnp.bfloat16),
        in_specs=[pl.BlockSpec(memory_space=pltpu.SMEM), hbm, hbm, hbm],
        out_specs=pl.BlockSpec(memory_space=pltpu.VMEM),
        scratch_shapes=[
            pltpu.VMEM((total, q_cols), jnp.bfloat16),
            pltpu.VMEM((n_ctx, 2, total, kv_cols), jnp.bfloat16),
            pltpu.VMEM((pieces, kv_heads, per_kv * pair * rows, 2 * HEAD_WIDTH), jnp.float32),
            dma((n_head,)), dma((n_head,)), dma((n_head,)),
            dma((n_head,)), dma((n_head,)), dma((n_head,)),
            dma((3,)),
            dma((n_ctx, pieces)), dma((n_ctx, pieces)), dma((n_ctx, pieces)),
        ],
        compiler_params=pltpu.CompilerParams(
            collective_id=0, has_side_effects=True, vmem_limit_bytes=60 * 1024 * 1024
        ),
    )(block_order, query, key, value)


def solution(mesh):
    placed = (P(("ctx", "head"), None), P(("ctx", "head"), None), P(("ctx", "head"), None), P())
    return jax.shard_map(
        functools.partial(shards, mesh.shape["head"], mesh.shape["ctx"]),
        mesh=mesh, in_specs=placed, out_specs=P("ctx", "head"), check_vma=False,
    )
```

profile of v0, /device:TPU:0, one launch (start us, length us, event | category | flops | bytes accessed | tf_op | source)
XLA Modules:
  0.0 51.9 jit_solution(18380598200049449466)
XLA Ops:
  0.0 49.8 %shard_map.46 = bf16[768,512]{1,0:T(8,128)(2,1)} custom-call(s32[8]{0:T(128)} %order.1, bf16[96,4096]{1,0:T(8,128)(2,1)} %query.1, bf16[96,2048]{1,0:T(8,128)(2,1)} %key.1, bf16[96,2048]{1,0:T(8,128)(2,1)} %value.1), custom_call_target="tpu_custom_call" | custom-call | tf_op jit(solution)/shard_map/pallas_call | solution.py:257
  49.8 2.1 %copy.6 = bf16[768,512]{1,0:T(8,128)(2,1)} copy(bf16[768,512]{1,0:T(8,128)(2,1)} %shard_map.46) | data formatting | bytes 1572864
where the time goes:
time: 52.2 us; the launch traced here: 51.9 us
  Pallas kernels  49.8 us (95%)
  local copies, waits for them, and re-layouts  2.06 us (4%)
    pallas_call x1, Pallas kernels, shards(): pl.pallas_call(functools.partial(kernel, n_head, n_ctx, pair), out_shape=...  49.8 us
    unnamed x1, local copies, waits for them, and re-layouts  2.06 us

commit v1 on v0

v1 whole, which is shorter than its diff:
```python
import functools
import math

import jax
import jax.numpy as jnp
from jax import lax
from jax.experimental import pallas as pl
from jax.experimental.pallas import tpu as pltpu
from jax.sharding import PartitionSpec as P

HEAD_WIDTH = 128
MESH = pl.DeviceIdType.MESH
CAP = 50.0
IN_SCALE = 1.0 / (12.0 * CAP)
OUT_SCALE = CAP * math.log2(math.e)
HIDDEN = -4096.0


def flip(index, step, size):
    out, bit = 0, 1
    while bit < size:
        mine = (index // bit) % 2
        turn = (step // bit) % 2
        out = out + (mine + turn - 2 * mine * turn) * bit
        bit *= 2
    return out


def kernel(
    n_head, n_ctx, pair,
    order, query, key, value, out,
    qbuf, kv, acc,
    q_send, k_send, v_send, q_recv, k_recv, v_recv,
    local_sem, x_send, p_send, f_recv,
):
    me = lax.axis_index("head")
    ctx = lax.axis_index("ctx")
    chip, core = ctx // 2, ctx % 2
    partner = chip * 2 + 1 - core
    chips = n_ctx // 2
    pieces = n_head // pair
    rows = query.shape[0]
    total = rows * n_head
    block = total // 2
    q_cols = query.shape[1] // n_head
    kv_cols = key.shape[1] // n_head
    kv_heads = kv_cols // HEAD_WIDTH
    per_kv = q_cols // kv_cols
    h_cols = per_kv * HEAD_WIDTH
    piece_rows = rows * pair
    near_pieces = pieces // 2
    near = n_head // 2
    home = me // pair
    near_half = home // near_pieces
    far_half = 1 - near_half
    inner = (home + home // near_pieces) % 2
    same_core = [((chip + t) % chips) * 2 + core for t in range(chips)]
    other_core = [((chip + t) % chips) * 2 + 1 - core for t in range(chips)]
    peers = [flip(me, j, n_head) for j in range(1, n_head)]

    barrier = pltpu.get_barrier_semaphore()
    for d in peers:
        pl.semaphore_signal(barrier, inc=1, device_id={"head": d}, device_id_type=MESH)
    for c in [partner] + same_core[1:]:
        pl.semaphore_signal(barrier, inc=1, device_id={"ctx": c}, device_id_type=MESH)
    def rows_of(s):
        return pl.ds(pl.multiple_of(s * rows, rows), rows)

    def cols_of(s, width):
        return pl.ds(pl.multiple_of(s * width, width), width)

    mine = [
        pltpu.make_async_copy(key.at[:, cols_of(me, kv_cols)], kv.at[ctx, 0, rows_of(me)], local_sem.at[0]),
        pltpu.make_async_copy(value.at[:, cols_of(me, kv_cols)], kv.at[ctx, 1, rows_of(me)], local_sem.at[1]),
        pltpu.make_async_copy(query.at[:, cols_of(me, q_cols)], qbuf.at[rows_of(me)], local_sem.at[2]),
    ]
    for copy in mine:
        copy.start()

    pl.semaphore_wait(barrier, n_head - 1 + chips)

    def kv_sends(d):
        return [
            pltpu.make_async_remote_copy(
                src_ref=src.at[:, cols_of(d, kv_cols)], dst_ref=kv.at[ctx, i, rows_of(me)],
                send_sem=send.at[d], recv_sem=recv.at[me],
                device_id={"head": d}, device_id_type=MESH,
            )
            for i, (src, send, recv) in enumerate(((key, k_send, k_recv), (value, v_send, v_recv)))
        ]

    def q_send_to(d, h):
        return pltpu.make_async_remote_copy(
            src_ref=query.at[:, cols_of(d * kv_heads + h, h_cols)],
            dst_ref=qbuf.at[rows_of(me), h * h_cols : (h + 1) * h_cols],
            send_sem=q_send.at[h, d], recv_sem=q_recv.at[h, me],
            device_id={"head": d}, device_id_type=MESH,
        )

    sends = [copy for d in peers[near - 1 :] for copy in kv_sends(d)]
    sends += [copy for d in peers[: near - 1] for copy in kv_sends(d)]
    sends += [q_send_to(d, h) for d in peers[: near - 1] for h in range(kv_heads)]
    turned = peers[near - 1 + near // 2 :] + peers[near - 1 : near - 1 + near // 2]
    sends += [q_send_to(d, h) for h in range(kv_heads) for d in turned]
    for copy in sends:
        copy.start()

    def arrived(ref, sem):
        pltpu.make_async_copy(ref, ref, sem).wait()

    def kv_ref(c, s):
        return kv.at[c, :, rows_of(s)]

    def pass_on(c, s, dest, send):
        copy = pltpu.make_async_remote_copy(
            src_ref=kv_ref(c, s), dst_ref=kv_ref(c, s),
            send_sem=send, recv_sem=f_recv.at[c, s],
            device_id={"ctx": dest}, device_id_type=MESH,
        )
        copy.start()

    def spread(j):
        s = flip(me, j, n_head)
        if isinstance(j, int) and j == 0:
            mine[0].wait()
            mine[1].wait()
        else:
            arrived(kv.at[ctx, 0, rows_of(s)], k_recv.at[s])
            arrived(kv.at[ctx, 1, rows_of(s)], v_recv.at[s])
        for c in same_core[1:]:
            pass_on(ctx, s, c, x_send.at[c, s])
        pass_on(ctx, s, partner, p_send.at[ctx, s])

    def relay(j):
        s = flip(me, j, n_head)
        for c in same_core[1:]:
            arrived(kv_ref(c, s), f_recv.at[c, s])
            pass_on(c, s, partner, p_send.at[c, s])

    def from_partner(j):
        s = flip(me, j, n_head)
        for c in other_core:
            arrived(kv_ref(c, s), f_recv.at[c, s])

    ones = jnp.ones((2 * block, HEAD_WIDTH), jnp.bfloat16)

    def unit(h, first_row, half, t, diagonal):
        q_half = first_row // block
        q_block = order[2 * ctx + q_half]
        c0 = ((chip + t) % chips) * 2 + core
        c1 = ((chip + t) % chips) * 2 + 1 - core
        q_span = pl.ds(pl.multiple_of(first_row, piece_rows), piece_rows)
        k_span = pl.ds(pl.multiple_of(half * block, block), block)
        low = jnp.where(order[2 * c0 + half] <= q_block, 0.0, HIDDEN)
        high = jnp.where(order[2 * c1 + half] <= q_block, 0.0, HIDDEN)
        cols = slice(h * HEAD_WIDTH, (h + 1) * HEAD_WIDTH)
        q = jnp.concatenate(
            [qbuf[q_span, (h * per_kv + i) * HEAD_WIDTH : (h * per_kv + i + 1) * HEAD_WIDTH] for i in range(per_kv)],
            axis=0,
        )
        k = jnp.concatenate([kv[c0, 0, k_span, cols], kv[c1, 0, k_span, cols]], axis=0)
        v = jnp.concatenate([kv[c0, 1, k_span, cols], kv[c1, 1, k_span, cols]], axis=0)
        x = lax.dot_general(q, k, (((1,), (1,)), ((), ())), preferred_element_type=jnp.float32)
        x = jnp.tanh(x * IN_SCALE) * OUT_SCALE
        if diagonal:
            q_at = first_row - q_half * block + lax.broadcasted_iota(jnp.int32, (piece_rows, block), 0)
            visible = lax.broadcasted_iota(jnp.int32, (piece_rows, block), 1) <= q_at
            e = jnp.exp2(x[:, :block]).reshape(per_kv, piece_rows, block)
            left = jnp.where(visible[None], e, 0.0).reshape(per_kv * piece_rows, block)
        else:
            left = jnp.exp2(x[:, :block] + low)
        w = jnp.concatenate([left, jnp.exp2(x[:, block:] + high)], axis=1).astype(jnp.bfloat16)
        return jnp.dot(w, jnp.concatenate([v, ones], axis=1), preferred_element_type=jnp.float32)

    def q_arrived(h, j):
        s = flip(me, j, n_head)
        arrived(qbuf.at[rows_of(s), h * h_cols : (h + 1) * h_cols], q_recv.at[h, s])

    def finish(h, first_row, at):
        span = pl.ds(pl.multiple_of(first_row, piece_rows), piece_rows)
        a = acc[at, h]
        o = (a[:, :HEAD_WIDTH] / a[:, HEAD_WIDTH:]).astype(jnp.bfloat16)
        for i in range(per_kv):
            col = (h * per_kv + i) * HEAD_WIDTH
            out[span, col : col + HEAD_WIDTH] = o[i * piece_rows : (i + 1) * piece_rows]

    def each(count, body):
        lax.fori_loop(0, count, lambda i, carry: (body(i), carry)[1], 0)

    near_steps = range(near_pieces)
    far_steps = [near_pieces + flip(1 - inner, k, near_pieces) for k in near_steps]

    def far_peers(k):
        return [far_steps[k] * pair + t for t in range(pair)]

    def near_near(step):
        for t in range(pair):
            j = step * pair + t
            if step + t == 0:
                mine[2].wait()
            else:
                for h in range(kv_heads):
                    q_arrived(h, j)
        first_row = flip(home, step, pieces) * piece_rows
        for h in range(kv_heads):
            acc[step, h] = unit(h, first_row, near_half, 0, True)

        def more(t):
            for h in range(kv_heads):
                acc[step, h] += unit(h, first_row, near_half, t + 1, False)

        each(chips - 1, more)

    for j in range(pair):
        spread(j)

    @pl.when(inner == 0)
    def _():
        for j in range(pair, near):
            spread(j)

    for j in far_peers(0):
        spread(j)

    @pl.when(inner == 1)
    def _():
        for j in range(pair, near):
            spread(j)

    for k in near_steps[1:]:
        for j in far_peers(k):
            spread(j)
    for j in range(near):
        relay(j)
    for j in range(near):
        from_partner(j)
    near_near(0)
    for j in far_peers(0):
        relay(j)
    for step in near_steps[1:]:
        near_near(step)
    for k in near_steps[1:]:
        for j in far_peers(k):
            relay(j)
    for k in near_steps:
        for j in far_peers(k):
            from_partner(j)

    def rest(step):
        first_row = flip(home, step, pieces) * piece_rows
        def more(t):
            for h in range(kv_heads):
                acc[step, h] += unit(h, first_row, far_half, t, False)

        each(chips, more)
        for h in range(kv_heads):
            finish(h, first_row, step)

    each(near_pieces, rest)

    for h in range(kv_heads):
        def far_all(k):
            step = near_pieces + flip(1 - inner, k, near_pieces)
            for t in range(pair):
                q_arrived(h, step * pair + t)
            first_row = flip(home, step, pieces) * piece_rows
            acc[near_pieces, h] = unit(h, first_row, far_half, 0, True) + unit(h, first_row, near_half, 0, False)

            def more(t):
                acc[near_pieces, h] += unit(h, first_row, far_half, t + 1, False) + unit(h, first_row, near_half, t + 1, False)

            each(chips - 1, more)
            finish(h, first_row, near_pieces)

        each(near_pieces, far_all)
    for copy in sends:
        copy.wait_send()
    for s in range(n_head):
        for c in same_core:
            arrived(kv_ref(c, s), p_send.at[c, s])
        for c in same_core[1:]:
            arrived(kv_ref(ctx, s), x_send.at[c, s])


def shards(n_head, n_ctx, query, key, value, block_order):
    rows = query.shape[0]
    total = rows * n_head
    q_cols = query.shape[1] // n_head
    kv_cols = key.shape[1] // n_head
    kv_heads = kv_cols // HEAD_WIDTH
    per_kv = q_cols // kv_cols
    pair = 2
    pieces = n_head // pair
    hbm = pl.BlockSpec(memory_space=pltpu.HBM)
    dma = pltpu.SemaphoreType.DMA
    return pl.pallas_call(
        functools.partial(kernel, n_head, n_ctx, pair),
        out_shape=jax.ShapeDtypeStruct((total, q_cols), jnp.bfloat16),
        in_specs=[pl.BlockSpec(memory_space=pltpu.SMEM), hbm, hbm, hbm],
        out_specs=pl.BlockSpec(memory_space=pltpu.VMEM),
        scratch_shapes=[
            pltpu.VMEM((total, q_cols), jnp.bfloat16),
            pltpu.VMEM((n_ctx, 2, total, kv_cols), jnp.bfloat16),
            pltpu.VMEM((pieces // 2 + 1, kv_heads, per_kv * pair * rows, 2 * HEAD_WIDTH), jnp.float32),
            dma((kv_heads, n_head)), dma((n_head,)), dma((n_head,)),
            dma((kv_heads, n_head)), dma((n_head,)), dma((n_head,)),
            dma((3,)),
            dma((n_ctx, n_head)), dma((n_ctx, n_head)), dma((n_ctx, n_head)),
        ],
        compiler_params=pltpu.CompilerParams(
            collective_id=0, has_side_effects=True, vmem_limit_bytes=60 * 1024 * 1024
        ),
    )(block_order, query, key, value)


def solution(mesh):
    placed = (P(("ctx", "head"), None), P(("ctx", "head"), None), P(("ctx", "head"), None), P())
    return jax.shard_map(
        functools.partial(shards, mesh.shape["head"], mesh.shape["ctx"]),
        mesh=mesh, in_specs=placed, out_specs=P("ctx", "head"), check_vma=False,
    )
```

time: 52.2 us -> 48.8 us (0.935)
  Pallas kernels: 49.8 us -> 46.5 us
    pallas_call x1, Pallas kernels: 49.8 us -> 46.5 us  [shards(): pl.pallas_call(functools.partial(kernel, n_head, n_ctx, pair), out_shape=...]
where the time goes in v1:
time: 48.8 us; the launch traced here: 48.6 us
  Pallas kernels  46.5 us (95%)
  local copies, waits for them, and re-layouts  2.06 us (4%)
    pallas_call x1, Pallas kernels, shards(): pl.pallas_call(functools.partial(kernel, n_head, n_ctx, pair), out_shape=...  46.5 us
    unnamed x1, local copies, waits for them, and re-layouts  2.06 us

profile of v1, /device:TPU:0, one launch (start us, length us, event | category | flops | bytes accessed | tf_op | source)
XLA Modules:
  0.0 48.6 jit_solution(2725238051682122864)
XLA Ops:
  0.0 46.5 %shard_map.46 = bf16[768,512]{1,0:T(8,128)(2,1)} custom-call(s32[8]{0:T(128)} %order.1, bf16[96,4096]{1,0:T(8,128)(2,1)} %query.1, bf16[96,2048]{1,0:T(8,128)(2,1)} %key.1, bf16[96,2048]{1,0:T(8,128)(2,1)} %value.1), custom_call_target="tpu_custom_call" | custom-call | tf_op jit(solution)/shard_map/pallas_call | solution.py:296
  46.5 2.1 %copy.6 = bf16[768,512]{1,0:T(8,128)(2,1)} copy(bf16[768,512]{1,0:T(8,128)(2,1)} %shard_map.46) | data formatting | bytes 1572864

commit v2 on v1

--- a/solution.py
+++ b/solution.py
@@ -30,8 +30,8 @@
     n_head, n_ctx, pair,
     order, query, key, value, out,
     qbuf, kv, acc,
-    q_send, k_send, v_send, q_recv, k_recv, v_recv,
-    local_sem, x_send, p_send, f_recv,
+    q_sent, kv_sent, x_sent, p_sent,
+    q_recv, kv_recv, x_recv, p_recv, local_sem,
 ):
     me = lax.axis_index("head")
     ctx = lax.axis_index("ctx")
@@ -71,8 +71,8 @@
 
     mine = [
         pltpu.make_async_copy(key.at[:, cols_of(me, kv_cols)], kv.at[ctx, 0, rows_of(me)], local_sem.at[0]),
-        pltpu.make_async_copy(value.at[:, cols_of(me, kv_cols)], kv.at[ctx, 1, rows_of(me)], local_sem.at[1]),
-        pltpu.make_async_copy(query.at[:, cols_of(me, q_cols)], qbuf.at[rows_of(me)], local_sem.at[2]),
+        pltpu.make_async_copy(value.at[:, cols_of(me, kv_cols)], kv.at[ctx, 1, rows_of(me)], local_sem.at[0]),
+        pltpu.make_async_copy(query.at[:, cols_of(me, q_cols)], qbuf.at[rows_of(me)], local_sem.at[1]),
     ]
     for copy in mine:
         copy.start()
@@ -83,25 +83,25 @@
         return [
             pltpu.make_async_remote_copy(
                 src_ref=src.at[:, cols_of(d, kv_cols)], dst_ref=kv.at[ctx, i, rows_of(me)],
-                send_sem=send.at[d], recv_sem=recv.at[me],
+                send_sem=kv_sent, recv_sem=kv_recv.at[me],
                 device_id={"head": d}, device_id_type=MESH,
             )
-            for i, (src, send, recv) in enumerate(((key, k_send, k_recv), (value, v_send, v_recv)))
+            for i, src in enumerate((key, value))
         ]
 
-    def q_send_to(d, h):
+    def q_send(d, h, heads):
         return pltpu.make_async_remote_copy(
-            src_ref=query.at[:, cols_of(d * kv_heads + h, h_cols)],
-            dst_ref=qbuf.at[rows_of(me), h * h_cols : (h + 1) * h_cols],
-            send_sem=q_send.at[h, d], recv_sem=q_recv.at[h, me],
+            src_ref=query.at[:, pl.ds(pl.multiple_of(d * q_cols + h * h_cols, h_cols), heads * h_cols)],
+            dst_ref=qbuf.at[rows_of(me), h * h_cols : (h + heads) * h_cols],
+            send_sem=q_sent, recv_sem=q_recv.at[h, me // pair],
             device_id={"head": d}, device_id_type=MESH,
         )
 
     sends = [copy for d in peers[near - 1 :] for copy in kv_sends(d)]
     sends += [copy for d in peers[: near - 1] for copy in kv_sends(d)]
-    sends += [q_send_to(d, h) for d in peers[: near - 1] for h in range(kv_heads)]
-    turned = peers[near - 1 + near // 2 :] + peers[near - 1 : near - 1 + near // 2]
-    sends += [q_send_to(d, h) for h in range(kv_heads) for d in turned]
+    sends += [q_send(d, 0, kv_heads) for d in peers[: near - 1]]
+    ordered = [far_half * near + i // pair * pair + flip(me % pair, i % pair, pair) for i in range(near)]
+    sends += [q_send(d, h, 1) for h in range(kv_heads) for d in ordered]
     for copy in sends:
         copy.start()
 
@@ -111,36 +111,34 @@
     def kv_ref(c, s):
         return kv.at[c, :, rows_of(s)]
 
-    def pass_on(c, s, dest, send):
+    def pass_on(c, s, dest, send, recv):
         copy = pltpu.make_async_remote_copy(
             src_ref=kv_ref(c, s), dst_ref=kv_ref(c, s),
-            send_sem=send, recv_sem=f_recv.at[c, s],
+            send_sem=send, recv_sem=recv,
             device_id={"ctx": dest}, device_id_type=MESH,
         )
         copy.start()
 
+    def to_partner(c, s):
+        pass_on(c, s, partner, p_sent, p_recv.at[c // 2, s // near])
+
     def spread(j):
         s = flip(me, j, n_head)
-        if isinstance(j, int) and j == 0:
-            mine[0].wait()
-            mine[1].wait()
-        else:
-            arrived(kv.at[ctx, 0, rows_of(s)], k_recv.at[s])
-            arrived(kv.at[ctx, 1, rows_of(s)], v_recv.at[s])
+        arrived(kv_ref(ctx, s), local_sem.at[0] if isinstance(j, int) and j == 0 else kv_recv.at[s])
         for c in same_core[1:]:
-            pass_on(ctx, s, c, x_send.at[c, s])
-        pass_on(ctx, s, partner, p_send.at[ctx, s])
+            pass_on(ctx, s, c, x_sent, x_recv.at[chip, s])
+        to_partner(ctx, s)
 
     def relay(j):
         s = flip(me, j, n_head)
         for c in same_core[1:]:
-            arrived(kv_ref(c, s), f_recv.at[c, s])
-            pass_on(c, s, partner, p_send.at[c, s])
-
-    def from_partner(j):
-        s = flip(me, j, n_head)
+            arrived(kv_ref(c, s), x_recv.at[c // 2, s])
+            to_partner(c, s)
+
+    def from_partner(half):
         for c in other_core:
-            arrived(kv_ref(c, s), f_recv.at[c, s])
+            span = pl.ds(pl.multiple_of(half * block, block), block)
+            arrived(kv.at[c, :, span], p_recv.at[c // 2, half])
 
     ones = jnp.ones((2 * block, HEAD_WIDTH), jnp.bfloat16)
 
@@ -172,9 +170,14 @@
         w = jnp.concatenate([left, jnp.exp2(x[:, block:] + high)], axis=1).astype(jnp.bfloat16)
         return jnp.dot(w, jnp.concatenate([v, ones], axis=1), preferred_element_type=jnp.float32)
 
-    def q_arrived(h, j):
-        s = flip(me, j, n_head)
-        arrived(qbuf.at[rows_of(s), h * h_cols : (h + 1) * h_cols], q_recv.at[h, s])
+    def q_arrived(step, h, heads):
+        p = flip(home, step, pieces)
+        count = pair
+        first = p * pair
+        if isinstance(step, int) and step == 0:
+            mine[2].wait()
+            first, count = flip(me, 1, n_head), pair - 1
+        arrived(qbuf.at[pl.ds(pl.multiple_of(first * rows, rows), count * rows), h * h_cols : (h + heads) * h_cols], q_recv.at[h, p])
 
     def finish(h, first_row, at):
         span = pl.ds(pl.multiple_of(first_row, piece_rows), piece_rows)
@@ -194,13 +197,7 @@
         return [far_steps[k] * pair + t for t in range(pair)]
 
     def near_near(step):
-        for t in range(pair):
-            j = step * pair + t
-            if step + t == 0:
-                mine[2].wait()
-            else:
-                for h in range(kv_heads):
-                    q_arrived(h, j)
+        q_arrived(step, 0, kv_heads)
         first_row = flip(home, step, pieces) * piece_rows
         for h in range(kv_heads):
             acc[step, h] = unit(h, first_row, near_half, 0, True)
@@ -232,8 +229,7 @@
             spread(j)
     for j in range(near):
         relay(j)
-    for j in range(near):
-        from_partner(j)
+    from_partner(near_half)
     near_near(0)
     for j in far_peers(0):
         relay(j)
@@ -242,9 +238,7 @@
     for k in near_steps[1:]:
         for j in far_peers(k):
             relay(j)
-    for k in near_steps:
-        for j in far_peers(k):
-            from_partner(j)
+    from_partner(far_half)
 
     def rest(step):
         first_row = flip(home, step, pieces) * piece_rows
@@ -261,8 +255,7 @@
     for h in range(kv_heads):
         def far_all(k):
             step = near_pieces + flip(1 - inner, k, near_pieces)
-            for t in range(pair):
-                q_arrived(h, step * pair + t)
+            q_arrived(step, h, 1)
             first_row = flip(home, step, pieces) * piece_rows
             acc[near_pieces, h] = unit(h, first_row, far_half, 0, True) + unit(h, first_row, near_half, 0, False)
 
@@ -273,13 +266,11 @@
             finish(h, first_row, near_pieces)
 
         each(near_pieces, far_all)
-    for copy in sends:
-        copy.wait_send()
-    for s in range(n_head):
-        for c in same_core:
-            arrived(kv_ref(c, s), p_send.at[c, s])
-        for c in same_core[1:]:
-            arrived(kv_ref(ctx, s), x_send.at[c, s])
+    arrived(kv.at[ctx, :, : (n_head - 1) * rows], kv_sent)
+    arrived(qbuf.at[: (n_head - 1) * rows], q_sent)
+    if chips > 1:
+        arrived(kv.at[: chips - 1], x_sent)
+    arrived(kv.at[:chips], p_sent)
 
 
 def shards(n_head, n_ctx, query, key, value, block_order):
@@ -295,17 +286,15 @@
     dma = pltpu.SemaphoreType.DMA
     return pl.pallas_call(
         functools.partial(kernel, n_head, n_ctx, pair),
-        out_shape=jax.ShapeDtypeStruct((total, q_cols), jnp.bfloat16),
+        out_shape=pltpu.VMEM((total, q_cols), jnp.bfloat16),
         in_specs=[pl.BlockSpec(memory_space=pltpu.SMEM), hbm, hbm, hbm],
         out_specs=pl.BlockSpec(memory_space=pltpu.VMEM),
         scratch_shapes=[
             pltpu.VMEM((total, q_cols), jnp.bfloat16),
             pltpu.VMEM((n_ctx, 2, total, kv_cols), jnp.bfloat16),
             pltpu.VMEM((pieces // 2 + 1, kv_heads, per_kv * pair * rows, 2 * HEAD_WIDTH), jnp.float32),
-            dma((kv_heads, n_head)), dma((n_head,)), dma((n_head,)),
-            dma((kv_heads, n_head)), dma((n_head,)), dma((n_head,)),
-            dma((3,)),
-            dma((n_ctx, n_head)), dma((n_ctx, n_head)), dma((n_ctx, n_head)),
+            dma(()), dma(()), dma(()), dma(()),
+            dma((kv_heads, pieces)), dma((n_head,)), dma((n_ctx // 2, n_head)), dma((n_ctx // 2, 2)), dma((2,)),
         ],
         compiler_params=pltpu.CompilerParams(
             collective_id=0, has_side_effects=True, vmem_limit_bytes=60 * 1024 * 1024

time: 48.8 us -> 43.9 us (0.90)
  Pallas kernels: 46.5 us -> 42.8 us
  local copies, waits for them, and re-layouts: 2.06 us -> 0.88 us
    pallas_call x1, Pallas kernels: 46.5 us -> 42.8 us  [shards(): pl.pallas_call(functools.partial(kernel, n_head, n_ctx, pair), out_shape=...]
    unnamed x1, local copies, waits for them, and re-layouts: 2.06 us -> 0.88 us
where the time goes in v2:
time: 43.9 us; the launch traced here: 43.7 us
  Pallas kernels  42.8 us (97%)
  local copies, waits for them, and re-layouts  0.88 us (2%)
    pallas_call x1, Pallas kernels, shards(): pl.pallas_call(functools.partial(kernel, n_head, n_ctx, pair), out_shape=...  42.8 us
    unnamed x1, local copies, waits for them, and re-layouts  0.88 us

profile of v2, /device:TPU:0, one launch (start us, length us, event | category | flops | bytes accessed | tf_op | source)
XLA Modules:
  0.0 43.7 jit_solution(11065434626742020386)
XLA Ops:
  0.0 42.8 %shard_map.46 = bf16[768,512]{1,0:T(8,128)(2,1)S(1)} custom-call(s32[8]{0:T(128)} %order.1, bf16[96,4096]{1,0:T(8,128)(2,1)} %query.1, bf16[96,2048]{1,0:T(8,128)(2,1)} %key.1, bf16[96,2048]{1,0:T(8,128)(2,1)} %value.1), custom_call_target="tpu_custom_call" | custom-call | tf_op jit(solution)/shard_map/pallas_call | solution.py:287
  42.9 0.9 %copy.6 = bf16[768,512]{1,0:T(8,128)(2,1)} copy(bf16[768,512]{1,0:T(8,128)(2,1)S(1)} %shard_map.46) | data formatting | bytes 1572864

commit v3 on v2

--- a/solution.py
+++ b/solution.py
@@ -32,6 +32,7 @@
     qbuf, kv, acc,
     q_sent, kv_sent, x_sent, p_sent,
     q_recv, kv_recv, x_recv, p_recv, local_sem,
+    head_ready, ctx_ready,
 ):
     me = lax.axis_index("head")
     ctx = lax.axis_index("ctx")
@@ -58,11 +59,24 @@
     other_core = [((chip + t) % chips) * 2 + 1 - core for t in range(chips)]
     peers = [flip(me, j, n_head) for j in range(1, n_head)]
 
+    others = [("head", d) for d in peers] + [("ctx", c) for c in [partner] + same_core[1:]]
+    at = {"head": me, "ctx": ctx}
+    ready = {"head": head_ready, "ctx": ctx_ready}
+
+    def tell(sem, axis, d):
+        pl.semaphore_signal(sem, inc=1, device_id={axis: d}, device_id_type=MESH)
+
+    def met(axis, d):
+        @pl.when(d > at[axis])
+        def _():
+            pl.semaphore_wait(ready[axis].at[d], 1)
+
     barrier = pltpu.get_barrier_semaphore()
-    for d in peers:
-        pl.semaphore_signal(barrier, inc=1, device_id={"head": d}, device_id_type=MESH)
-    for c in [partner] + same_core[1:]:
-        pl.semaphore_signal(barrier, inc=1, device_id={"ctx": c}, device_id_type=MESH)
+    for axis, d in others:
+        @pl.when(d > at[axis])
+        def _():
+            tell(barrier, axis, d)
+
     def rows_of(s):
         return pl.ds(pl.multiple_of(s * rows, rows), rows)
 
@@ -77,7 +91,15 @@
     for copy in mine:
         copy.start()
 
-    pl.semaphore_wait(barrier, n_head - 1 + chips)
+    @pl.when(me + chip + core > 0)
+    def _():
+        pl.semaphore_wait(barrier, me + chip + core)
+
+    for axis, d in others:
+        @pl.when(d < at[axis])
+        def _():
+            tell(ready[axis].at[at[axis]], axis, d)
+
 
     def kv_sends(d):
         return [
@@ -97,14 +119,6 @@
             device_id={"head": d}, device_id_type=MESH,
         )
 
-    sends = [copy for d in peers[near - 1 :] for copy in kv_sends(d)]
-    sends += [copy for d in peers[: near - 1] for copy in kv_sends(d)]
-    sends += [q_send(d, 0, kv_heads) for d in peers[: near - 1]]
-    ordered = [far_half * near + i // pair * pair + flip(me % pair, i % pair, pair) for i in range(near)]
-    sends += [q_send(d, h, 1) for h in range(kv_heads) for d in ordered]
-    for copy in sends:
-        copy.start()
-
     def arrived(ref, sem):
         pltpu.make_async_copy(ref, ref, sem).wait()
 
@@ -140,14 +154,48 @@
             span = pl.ds(pl.multiple_of(half * block, block), block)
             arrived(kv.at[c, :, span], p_recv.at[c // 2, half])
 
+    near_js, far_js = list(range(1, near)), list(range(near, n_head))
+
+    def send_kv(js):
+        for j in js:
+            met("head", peers[j - 1])
+            for copy in kv_sends(peers[j - 1]):
+                copy.start()
+
+    @pl.when(near_half == 1)
+    def _():
+        send_kv(far_js)
+
+    for c in [partner] + same_core[1:]:
+        met("ctx", c)
+    spread(0)
+
+    @pl.when(near_half == 1)
+    def _():
+        send_kv(near_js)
+
+    @pl.when((near_half == 0) & (inner == 0))
+    def _():
+        send_kv(near_js[: pair - 1] + far_js[: near // 2] + near_js[pair - 1 :] + far_js[near // 2 :])
+
+    @pl.when((near_half == 0) & (inner == 1))
+    def _():
+        send_kv(far_js[near // 2 :] + near_js + far_js[: near // 2])
+
+    ordered = [far_half * near + i // pair * pair + flip(me % pair, i % pair, pair) for i in range(near)]
+    sends = [q_send(d, 0, kv_heads) for d in peers[: near - 1]]
+    sends += [q_send(d, h, 1) for h in range(kv_heads) for d in ordered]
+    for copy in sends:
+        copy.start()
+
     ones = jnp.ones((2 * block, HEAD_WIDTH), jnp.bfloat16)
 
-    def unit(h, first_row, half, t, diagonal):
+    def unit(h, first_row, m, half, t, diagonal):
         q_half = first_row // block
         q_block = order[2 * ctx + q_half]
         c0 = ((chip + t) % chips) * 2 + core
         c1 = ((chip + t) % chips) * 2 + 1 - core
-        q_span = pl.ds(pl.multiple_of(first_row, piece_rows), piece_rows)
+        q_span = pl.ds(pl.multiple_of(first_row, piece_rows), m)
         k_span = pl.ds(pl.multiple_of(half * block, block), block)
         low = jnp.where(order[2 * c0 + half] <= q_block, 0.0, HIDDEN)
         high = jnp.where(order[2 * c1 + half] <= q_block, 0.0, HIDDEN)
@@ -161,10 +209,10 @@
         x = lax.dot_general(q, k, (((1,), (1,)), ((), ())), preferred_element_type=jnp.float32)
         x = jnp.tanh(x * IN_SCALE) * OUT_SCALE
         if diagonal:
-            q_at = first_row - q_half * block + lax.broadcasted_iota(jnp.int32, (piece_rows, block), 0)
-            visible = lax.broadcasted_iota(jnp.int32, (piece_rows, block), 1) <= q_at
-            e = jnp.exp2(x[:, :block]).reshape(per_kv, piece_rows, block)
-            left = jnp.where(visible[None], e, 0.0).reshape(per_kv * piece_rows, block)
+            q_at = first_row - q_half * block + lax.broadcasted_iota(jnp.int32, (m, block), 0)
+            visible = lax.broadcasted_iota(jnp.int32, (m, block), 1) <= q_at
+            e = jnp.exp2(x[:, :block]).reshape(per_kv, m, block)
+            left = jnp.where(visible[None], e, 0.0).reshape(per_kv * m, block)
         else:
             left = jnp.exp2(x[:, :block] + low)
         w = jnp.concatenate([left, jnp.exp2(x[:, block:] + high)], axis=1).astype(jnp.bfloat16)
@@ -179,13 +227,12 @@
             first, count = flip(me, 1, n_head), pair - 1
         arrived(qbuf.at[pl.ds(pl.multiple_of(first * rows, rows), count * rows), h * h_cols : (h + heads) * h_cols], q_recv.at[h, p])
 
-    def finish(h, first_row, at):
-        span = pl.ds(pl.multiple_of(first_row, piece_rows), piece_rows)
-        a = acc[at, h]
+    def finish(h, first_row, m, a):
+        span = pl.ds(pl.multiple_of(first_row, piece_rows), m)
         o = (a[:, :HEAD_WIDTH] / a[:, HEAD_WIDTH:]).astype(jnp.bfloat16)
         for i in range(per_kv):
             col = (h * per_kv + i) * HEAD_WIDTH
-            out[span, col : col + HEAD_WIDTH] = o[i * piece_rows : (i + 1) * piece_rows]
+            out[span, col : col + HEAD_WIDTH] = o[i * m : (i + 1) * m]
 
     def each(count, body):
         lax.fori_loop(0, count, lambda i, carry: (body(i), carry)[1], 0)
@@ -196,19 +243,23 @@
     def far_peers(k):
         return [far_steps[k] * pair + t for t in range(pair)]
 
-    def near_near(step):
-        q_arrived(step, 0, kv_heads)
-        first_row = flip(home, step, pieces) * piece_rows
-        for h in range(kv_heads):
-            acc[step, h] = unit(h, first_row, near_half, 0, True)
+    near_row, far_row = near_half * block, far_half * block
+
+    def add_up(h, first_row, m, halves, diagonal, start):
+        a = acc.at[h, : per_kv * m]
+        o = sum(unit(h, first_row, m, half, 0, diagonal and half is halves[0]) for half in halves)
+        a[...] = o if start else a[...] + o
 
         def more(t):
-            for h in range(kv_heads):
-                acc[step, h] += unit(h, first_row, near_half, t + 1, False)
+            a[...] += sum(unit(h, first_row, m, half, t + 1, False) for half in halves)
 
         each(chips - 1, more)
 
-    for j in range(pair):
+    def pass_far(k):
+        for j in far_peers(k):
+            relay(j)
+
+    for j in range(1, pair):
         spread(j)
 
     @pl.when(inner == 0)
@@ -229,43 +280,37 @@
             spread(j)
     for j in range(near):
         relay(j)
+
+    @pl.when(core == 1)
+    def _():
+        for k in near_steps[:-1]:
+            pass_far(k)
+
     from_partner(near_half)
-    near_near(0)
-    for j in far_peers(0):
-        relay(j)
-    for step in near_steps[1:]:
-        near_near(step)
-    for k in near_steps[1:]:
-        for j in far_peers(k):
-            relay(j)
+    for step in near_steps:
+        q_arrived(step, 0, kv_heads)
+    for h in range(kv_heads):
+        add_up(h, near_row, block, [near_half], True, True)
+        if h == 0:
+            @pl.when(core == 0)
+            def _():
+                for k in near_steps[:-1]:
+                    pass_far(k)
+
+            pass_far(near_pieces - 1)
     from_partner(far_half)
-
-    def rest(step):
-        first_row = flip(home, step, pieces) * piece_rows
-        def more(t):
-            for h in range(kv_heads):
-                acc[step, h] += unit(h, first_row, far_half, t, False)
-
-        each(chips, more)
-        for h in range(kv_heads):
-            finish(h, first_row, step)
-
-    each(near_pieces, rest)
-
     for h in range(kv_heads):
-        def far_all(k):
+        add_up(h, near_row, block, [far_half], False, False)
+        finish(h, near_row, block, acc[h])
+    for h in range(kv_heads):
+        def far(k):
             step = near_pieces + flip(1 - inner, k, near_pieces)
             q_arrived(step, h, 1)
             first_row = flip(home, step, pieces) * piece_rows
-            acc[near_pieces, h] = unit(h, first_row, far_half, 0, True) + unit(h, first_row, near_half, 0, False)
-
-            def more(t):
-                acc[near_pieces, h] += unit(h, first_row, far_half, t + 1, False) + unit(h, first_row, near_half, t + 1, False)
-
-            each(chips - 1, more)
-            finish(h, first_row, near_pieces)
-
-        each(near_pieces, far_all)
+            add_up(h, first_row, piece_rows, [far_half, near_half], True, True)
+            finish(h, first_row, piece_rows, acc[h, : per_kv * piece_rows])
+
+        each(near_pieces, far)
     arrived(kv.at[ctx, :, : (n_head - 1) * rows], kv_sent)
     arrived(qbuf.at[: (n_head - 1) * rows], q_sent)
     if chips > 1:
@@ -292,9 +337,10 @@
         scratch_shapes=[
             pltpu.VMEM((total, q_cols), jnp.bfloat16),
             pltpu.VMEM((n_ctx, 2, total, kv_cols), jnp.bfloat16),
-            pltpu.VMEM((pieces // 2 + 1, kv_heads, per_kv * pair * rows, 2 * HEAD_WIDTH), jnp.float32),
+            pltpu.VMEM((kv_heads, per_kv * total // 2, 2 * HEAD_WIDTH), jnp.float32),
             dma(()), dma(()), dma(()), dma(()),
             dma((kv_heads, pieces)), dma((n_head,)), dma((n_ctx // 2, n_head)), dma((n_ctx // 2, 2)), dma((2,)),
+            pltpu.SemaphoreType.REGULAR((n_head,)), pltpu.SemaphoreType.REGULAR((n_ctx,)),
         ],
         compiler_params=pltpu.CompilerParams(
             collective_id=0, has_side_effects=True, vmem_limit_bytes=60 * 1024 * 1024

time: 43.9 us -> 43 us (0.979)
  Pallas kernels: 42.8 us -> 42 us
    pallas_call x1, Pallas kernels: 42.8 us -> 42 us  [shards(): pl.pallas_call(functools.partial(kernel, n_head, n_ctx, pair), out_shape=...]
where the time goes in v3:
time: 43 us; the launch traced here: 42.9 us
  Pallas kernels  42 us (98%)
  local copies, waits for them, and re-layouts  0.88 us (2%)
    pallas_call x1, Pallas kernels, shards(): pl.pallas_call(functools.partial(kernel, n_head, n_ctx, pair), out_shape=...  42 us
    unnamed x1, local copies, waits for them, and re-layouts  0.88 us

profile of v3, /device:TPU:0, one launch (start us, length us, event | category | flops | bytes accessed | tf_op | source)
XLA Modules:
  0.0 42.9 jit_solution(2110901178683220329)
XLA Ops:
  0.0 42.0 %shard_map.46 = bf16[768,512]{1,0:T(8,128)(2,1)S(1)} custom-call(s32[8]{0:T(128)} %order.1, bf16[96,4096]{1,0:T(8,128)(2,1)} %query.1, bf16[96,2048]{1,0:T(8,128)(2,1)} %key.1, bf16[96,2048]{1,0:T(8,128)(2,1)} %value.1), custom_call_target="tpu_custom_call" | custom-call | tf_op jit(solution)/shard_map/pallas_call | solution.py:332
  42.0 0.9 %copy.6 = bf16[768,512]{1,0:T(8,128)(2,1)} copy(bf16[768,512]{1,0:T(8,128)(2,1)S(1)} %shard_map.46) | data formatting | bytes 1572864

commit v4 on v3

--- a/solution.py
+++ b/solution.py
@@ -182,7 +182,7 @@
     def _():
         send_kv(far_js[near // 2 :] + near_js + far_js[: near // 2])
 
-    ordered = [far_half * near + i // pair * pair + flip(me % pair, i % pair, pair) for i in range(near)]
+    ordered = [far_half * near + i for i in range(near)]
     sends = [q_send(d, 0, kv_heads) for d in peers[: near - 1]]
     sends += [q_send(d, h, 1) for h in range(kv_heads) for d in ordered]
     for copy in sends:
@@ -259,10 +259,12 @@
         for j in far_peers(k):
             relay(j)
 
+    later = (inner == 1) | ((near_half == 0) & (core == 0))
+
     for j in range(1, pair):
         spread(j)
 
-    @pl.when(inner == 0)
+    @pl.when(jnp.logical_not(later))
     def _():
         for j in range(pair, near):
             spread(j)
@@ -270,7 +272,7 @@
     for j in far_peers(0):
         spread(j)
 
-    @pl.when(inner == 1)
+    @pl.when(later)
     def _():
         for j in range(pair, near):
             spread(j)

time: 43 us -> 42 us (0.977)
  Pallas kernels: 42 us -> 40.9 us
    pallas_call x1, Pallas kernels: 42 us -> 40.9 us  [shards(): pl.pallas_call(functools.partial(kernel, n_head, n_ctx, pair), out_shape=...]
where the time goes in v4:
time: 42 us; the launch traced here: 41.8 us
  Pallas kernels  40.9 us (97%)
  local copies, waits for them, and re-layouts  0.88 us (2%)
    pallas_call x1, Pallas kernels, shards(): pl.pallas_call(functools.partial(kernel, n_head, n_ctx, pair), out_shape=...  40.9 us
    unnamed x1, local copies, waits for them, and re-layouts  0.88 us

profile of v4, /device:TPU:0, one launch (start us, length us, event | category | flops | bytes accessed | tf_op | source)
XLA Modules:
  0.0 41.8 jit_solution(9089432348218424214)
XLA Ops:
  0.0 40.9 %shard_map.46 = bf16[768,512]{1,0:T(8,128)(2,1)S(1)} custom-call(s32[8]{0:T(128)} %order.1, bf16[96,4096]{1,0:T(8,128)(2,1)} %query.1, bf16[96,2048]{1,0:T(8,128)(2,1)} %key.1, bf16[96,2048]{1,0:T(8,128)(2,1)} %value.1), custom_call_target="tpu_custom_call" | custom-call | tf_op jit(solution)/shard_map/pallas_call | solution.py:334
  40.9 0.9 %copy.6 = bf16[768,512]{1,0:T(8,128)(2,1)} copy(bf16[768,512]{1,0:T(8,128)(2,1)S(1)} %shard_map.46) | data formatting | bytes 1572864

commit v5 on v4

--- a/solution.py
+++ b/solution.py
@@ -28,8 +28,8 @@
 
 def kernel(
     n_head, n_ctx, pair,
-    order, query, key, value, out,
-    qbuf, kv, acc,
+    block_order, query, key, value, out,
+    qbuf, kv, acc, order,
     q_sent, kv_sent, x_sent, p_sent,
     q_recv, kv_recv, x_recv, p_recv, local_sem,
     head_ready, ctx_ready,
@@ -88,6 +88,7 @@
         pltpu.make_async_copy(value.at[:, cols_of(me, kv_cols)], kv.at[ctx, 1, rows_of(me)], local_sem.at[0]),
         pltpu.make_async_copy(query.at[:, cols_of(me, q_cols)], qbuf.at[rows_of(me)], local_sem.at[1]),
     ]
+    mine.append(pltpu.make_async_copy(block_order, order, local_sem.at[2]))
     for copy in mine:
         copy.start()
 
@@ -291,6 +292,7 @@
     from_partner(near_half)
     for step in near_steps:
         q_arrived(step, 0, kv_heads)
+    mine[3].wait()
     for h in range(kv_heads):
         add_up(h, near_row, block, [near_half], True, True)
         if h == 0:
@@ -334,14 +336,15 @@
     return pl.pallas_call(
         functools.partial(kernel, n_head, n_ctx, pair),
         out_shape=pltpu.VMEM((total, q_cols), jnp.bfloat16),
-        in_specs=[pl.BlockSpec(memory_space=pltpu.SMEM), hbm, hbm, hbm],
+        in_specs=[hbm, hbm, hbm, hbm],
         out_specs=pl.BlockSpec(memory_space=pltpu.VMEM),
         scratch_shapes=[
             pltpu.VMEM((total, q_cols), jnp.bfloat16),
             pltpu.VMEM((n_ctx, 2, total, kv_cols), jnp.bfloat16),
             pltpu.VMEM((kv_heads, per_kv * total // 2, 2 * HEAD_WIDTH), jnp.float32),
+            pltpu.SMEM(block_order.shape, jnp.int32),
             dma(()), dma(()), dma(()), dma(()),
-            dma((kv_heads, pieces)), dma((n_head,)), dma((n_ctx // 2, n_head)), dma((n_ctx // 2, 2)), dma((2,)),
+            dma((kv_heads, pieces)), dma((n_head,)), dma((n_ctx // 2, n_head)), dma((n_ctx // 2, 2)), dma((3,)),
             pltpu.SemaphoreType.REGULAR((n_head,)), pltpu.SemaphoreType.REGULAR((n_ctx,)),
         ],
         compiler_params=pltpu.CompilerParams(

time: 42 us -> 41.3 us (0.983)
  Pallas kernels: 40.9 us -> 40.2 us
    pallas_call x1, Pallas kernels: 40.9 us -> 40.2 us  [shards(): pl.pallas_call(functools.partial(kernel, n_head, n_ctx, pair), out_shape=...]
where the time goes in v5:
time: 41.3 us; the launch traced here: 41.1 us
  Pallas kernels  40.2 us (97%)
  local copies, waits for them, and re-layouts  0.88 us (2%)
    pallas_call x1, Pallas kernels, shards(): pl.pallas_call(functools.partial(kernel, n_head, n_ctx, pair), out_shape=...  40.2 us
    unnamed x1, local copies, waits for them, and re-layouts  0.88 us

profile of v5, /device:TPU:0, one launch (start us, length us, event | category | flops | bytes accessed | tf_op | source)
XLA Modules:
  0.0 41.1 jit_solution(8100575995346820252)
XLA Ops:
  0.0 40.2 %shard_map.46 = bf16[768,512]{1,0:T(8,128)(2,1)S(1)} custom-call(s32[8]{0:T(128)} %block_order.1, bf16[96,4096]{1,0:T(8,128)(2,1)} %query.1, bf16[96,2048]{1,0:T(8,128)(2,1)} %key.1, bf16[96,2048]{1,0:T(8,128)(2,1)} %value.1), custom_call_target="tpu_custom_call" | custom-call | tf_op jit(solution)/shard_map/pallas_call | solution.py:336
  40.2 0.9 %copy.6 = bf16[768,512]{1,0:T(8,128)(2,1)} copy(bf16[768,512]{1,0:T(8,128)(2,1)S(1)} %shard_map.46) | data formatting | bytes 1572864

commit v6 on v5

--- a/solution.py
+++ b/solution.py
@@ -141,13 +141,13 @@
         s = flip(me, j, n_head)
         arrived(kv_ref(ctx, s), local_sem.at[0] if isinstance(j, int) and j == 0 else kv_recv.at[s])
         for c in same_core[1:]:
-            pass_on(ctx, s, c, x_sent, x_recv.at[chip, s])
+            pass_on(ctx, s, c, x_sent, x_recv.at[(chip - c // 2 + chips) % chips - 1, s])
         to_partner(ctx, s)
 
     def relay(j):
         s = flip(me, j, n_head)
         for c in same_core[1:]:
-            arrived(kv_ref(c, s), x_recv.at[c // 2, s])
+            arrived(kv_ref(c, s), x_recv.at[(c // 2 - chip + chips) % chips - 1, s])
             to_partner(c, s)
 
     def from_partner(half):
@@ -301,7 +301,14 @@
                 for k in near_steps[:-1]:
                     pass_far(k)
 
-            pass_far(near_pieces - 1)
+            @pl.when(core == 1)
+            def _():
+                pass_far(near_pieces - 1)
+
+    @pl.when(core == 0)
+    def _():
+        pass_far(near_pieces - 1)
+
     from_partner(far_half)
     for h in range(kv_heads):
         add_up(h, near_row, block, [far_half], False, False)
@@ -344,7 +351,7 @@
             pltpu.VMEM((kv_heads, per_kv * total // 2, 2 * HEAD_WIDTH), jnp.float32),
             pltpu.SMEM(block_order.shape, jnp.int32),
             dma(()), dma(()), dma(()), dma(()),
-            dma((kv_heads, pieces)), dma((n_head,)), dma((n_ctx // 2, n_head)), dma((n_ctx // 2, 2)), dma((3,)),
+            dma((kv_heads, pieces)), dma((n_head,)), dma((max(n_ctx // 2 - 1, 1), n_head)), dma((n_ctx // 2, 2)), dma((3,)),
             pltpu.SemaphoreType.REGULAR((n_head,)), pltpu.SemaphoreType.REGULAR((n_ctx,)),
         ],
         compiler_params=pltpu.CompilerParams(

time: 41.3 us -> 41.2 us (level)
  no operation moved by 1% of the time
where the time goes in v6:
time: 41.2 us; the launch traced here: 41 us
  Pallas kernels  40.1 us (97%)
  local copies, waits for them, and re-layouts  0.88 us (2%)
    pallas_call x1, Pallas kernels, shards(): pl.pallas_call(functools.partial(kernel, n_head, n_ctx, pair), out_shape=...  40.1 us
    unnamed x1, local copies, waits for them, and re-layouts  0.88 us

profile of v6, /device:TPU:0, one launch (start us, length us, event | category | flops | bytes accessed | tf_op | source)
XLA Modules:
  0.0 41.0 jit_solution(2765602267216858501)
XLA Ops:
  0.0 40.1 %shard_map.46 = bf16[768,512]{1,0:T(8,128)(2,1)S(1)} custom-call(s32[8]{0:T(128)} %block_order.1, bf16[96,4096]{1,0:T(8,128)(2,1)} %query.1, bf16[96,2048]{1,0:T(8,128)(2,1)} %key.1, bf16[96,2048]{1,0:T(8,128)(2,1)} %value.1), custom_call_target="tpu_custom_call" | custom-call | tf_op jit(solution)/shard_map/pallas_call | solution.py:343
  40.1 0.9 %copy.6 = bf16[768,512]{1,0:T(8,128)(2,1)} copy(bf16[768,512]{1,0:T(8,128)(2,1)S(1)} %shard_map.46) | data formatting | bytes 1572864
